TPU v7x, 128 devices: a whole 4x4x4 slice. The times are simulated.
128 devices in a mesh: row: 8 (over x, core), col: 16 (over z, y).
Axes of the slice: x: 4, y: 4, z: 4, core: 2. Of those that a mesh axis runs over, the one named last changes fastest.
Arguments:
- rhs: float32 [32, 1048576], P(None, ('row', 'col')), may hold values from -12.5 to 12.5
- near_blocks: bfloat16 [16384, 4, 4096], P(('row', 'col')), may hold values from -0.1875 to 0.1875
- near_offsets: int32 [16384, 4], P(('row', 'col')), may hold values from -4 to 4, as said below
- v_factor: bfloat16 [16384, 2048], P(('row', 'col')), may hold values from -0.75 to 0.75
- mix_col: bfloat16 [8, 128, 512, 512], P('row', 'col'), may hold values from -0.25 to 0.25
- mix_row: bfloat16 [8, 256, 256, 256], P('row', 'col'), may hold values from -0.375 to 0.375
- u_factor: bfloat16 [16384, 2048], P(('row', 'col')), may hold values from -0.75 to 0.75
Outputs:
- solution: float32 [32, 1048576], P(None, ('row', 'col'))
- residual: float32 [32, 1048576], P(None, ('row', 'col'))
Inputs may be any that keep to these rules, and one draw needn't show every extreme that they name: `near_offsets`: column 0 is 0; the other entries of a row are distinct and nonzero. In every aligned block of 128 rows some row holds -4 and some row holds 4.
All inputs are finite; a program needn't handle non-finite values.
Results may differ from a plain program's by a relative error of at most 0.0054.
Values may be sent and summed in bfloat16 or wider, within the bound.
A program may use at most 128 MiB of HBM per device.

v0:
```python
import jax
import jax.numpy as jnp
from jax import lax
from jax.experimental import pallas as pl
from jax.experimental.pallas import tpu as pltpu
from jax.sharding import PartitionSpec as P

LEAF = 64
RANK = 32
HALO = 4
LANES = 128
QUAD = LANES // RANK
BF16 = jnp.bfloat16
F32 = jnp.float32
MESH = pl.DeviceIdType.MESH


def iota(shape, dim):
    return lax.broadcasted_iota(jnp.int32, shape, dim)


def dot(a, b):
    return jnp.dot(a, b, preferred_element_type=F32)


def lanes_at(index, width):
    return pl.ds(pl.multiple_of(index * width, width), width)


def regroup(tiles, group):
    out = []
    for j in range(QUAD):
        made = None
        for c in range(QUAD):
            shift = (c - j) * RANK % LANES
            moved = pltpu.roll(tiles[c], shift, 1) if shift else tiles[c]
            made = moved if made is None else jnp.where(group == c, moved, made)
        out.append(made)
    return out


def kernel(
    offs, rhs_h, near_h, v_h, mixc_h, mixr_h, u_h, sol, res,
    rhs, near_raw, v_raw, mixc, mixr, u_raw,
    near_w, v_big, u_big, pick_near, pick_v, pick_u,
    xbf, xdup, w_one, w_two, q_two,
    zbuf, zrecv, tbuf, trecv, halo, part, sums,
    load_sem, halo_s, halo_r, z_s, z_r, t_s, t_r, sum_s, sum_r,
):
    n_row = lax.axis_size("row")
    n_col = lax.axis_size("col")
    total = n_row * n_col
    row = lax.axis_index("row")
    col = lax.axis_index("col")
    me = row * n_col + col
    count, width = rhs.shape
    leaves = width // LEAF
    nnear = offs.shape[1]
    slots = leaves // n_col
    sub = slots // n_row
    edge = HALO * LEAF

    loads = {}
    for at, (name, src, dst) in enumerate(
        (("v", v_h, v_raw), ("rhs", rhs_h, rhs), ("near", near_h, near_raw),
         ("mixc", mixc_h, mixc), ("mixr", mixr_h, mixr), ("u", u_h, u_raw))
    ):
        loads[name] = pltpu.make_async_copy(src, dst, load_sem.at[at])
        if name in ("v", "rhs"):
            loads[name].start()

    barrier = pltpu.get_barrier_semaphore()
    before = lax.rem(me + total - 1, total)
    after = lax.rem(me + 1, total)
    before_id = (before // n_col, lax.rem(before, n_col))
    after_id = (after // n_col, lax.rem(after, n_col))

    def col_id(step):
        return (row, lax.rem(col + step, n_col))

    def row_id(step):
        return (lax.rem(row + step, n_row), col)

    def any_id(step):
        other = lax.rem(me + step, total)
        return (other // n_col, lax.rem(other, n_col))

    def greet(step, carry):
        pl.semaphore_signal(barrier, inc=1, device_id=any_id(step), device_id_type=MESH)
        return carry

    lax.fori_loop(1, total, greet, 0)

    lane = iota((count, LANES), 1)
    low = lane < LEAF
    group = lane // RANK

    r = iota(pick_v.shape, 0)
    c = iota(pick_v.shape, 1)
    pick_v[...] = jnp.where((c % 16 == r // LEAF) & (c // 16 == r % LEAF // QUAD), 1.0, 0.0).astype(BF16)
    r = iota(pick_u.shape, 0)
    c = iota(pick_u.shape, 1)
    pick_u[...] = jnp.where((c % 16 == r // RANK) & (c // 16 == r % RANK // 2), 1.0, 0.0).astype(BF16)
    r = iota(pick_near.shape, 0)
    c = iota(pick_near.shape, 1)
    pick_near[...] = jnp.where((c % nnear == r // LEAF) & (c // nnear == r % LEAF // 2), 1.0, 0.0).astype(BF16)

    def prepare_v():
        loads["v"].wait()
        for name in ("near", "mixc", "mixr", "u"):
            loads[name].start()
        rr = iota((QUAD * LEAF, LANES), 0)
        gg = iota((QUAD * LEAF, LANES), 1) // RANK
        own = gg == rr % QUAD
        place = gg == rr // LEAF

        def block(b, carry):
            base = pl.multiple_of(b * 16, 16)
            rows = jnp.concatenate(
                [v_raw[pl.ds(base, 16), t * LANES:(t + 1) * LANES] for t in range(16)], axis=0
            )
            for q in range(4):
                size = QUAD * LEAF
                m = dot(pick_v[q * size:(q + 1) * size, :], rows)
                m = jnp.where(own, m, 0.0)
                m = m + pltpu.roll(m, RANK, 1)
                m = m + pltpu.roll(m, 2 * RANK, 1)
                at = pl.multiple_of(b * 16 * LEAF + q * size, size)
                v_big[pl.ds(at, size), :] = jnp.where(place, m, 0.0).astype(BF16)
            return carry

        lax.fori_loop(0, leaves // 16, block, 0)

    def prepare_u():
        loads["u"].wait()
        size = QUAD * RANK
        rr = iota((size, LANES), 0)
        half = iota((size, LANES), 1) // LEAF
        own = half == rr % 2
        place = (rr // RANK) - half

        def block(b, carry):
            base = pl.multiple_of(b * 16, 16)
            rows = jnp.concatenate(
                [u_raw[pl.ds(base, 16), t * LANES:(t + 1) * LANES] for t in range(16)], axis=0
            )
            for q in range(4):
                m = dot(pick_u[q * size:(q + 1) * size, :], rows)
                m = jnp.where(own, m, 0.0)
                m = m + pltpu.roll(m, LEAF, 1)
                at = pl.multiple_of(b * 16 * RANK + q * size, size)
                u_big[pl.ds(at, size), 0:LANES] = jnp.where(place == 0, m, 0.0).astype(BF16)
                u_big[pl.ds(at, size), LANES:2 * LANES] = jnp.where(place == 2, m, 0.0).astype(BF16)
            return carry

        lax.fori_loop(0, leaves // 16, block, 0)

    def prepare_near():
        loads["near"].wait()
        rr = iota((LEAF, LANES), 0)
        left = iota((LEAF, LANES), 1) < LEAF
        own = left == (rr % 2 == 0)
        size = nnear * LEAF // 2

        def block(b, carry):
            for k in range(2):
                twin = b * 4 + k * 2
                both = dot(
                    pick_near[...],
                    jnp.concatenate(
                        [near_raw[lanes_at(twin, size), :], near_raw[lanes_at(twin + 1, size), :]], axis=1
                    ),
                )
                for which in range(2):
                    m = both[:, which * LANES:(which + 1) * LANES]
                    for pair in range(nnear // 2):
                        a = m[2 * pair * LEAF:(2 * pair + 1) * LEAF]
                        d = m[(2 * pair + 1) * LEAF:(2 * pair + 2) * LEAF]
                        straight = jnp.where(own, jnp.where(left, a, d), 0.0)
                        crossed = jnp.where(own, jnp.where(left, d, a), 0.0)
                        made = straight + pltpu.roll(crossed, LEAF, 1)
                        near_w[lanes_at(twin + which, LEAF), pair * LANES:(pair + 1) * LANES] = made.astype(BF16)
            return carry

        lax.fori_loop(0, leaves // 4, block, 0)

    def spread(tile, first):
        turned = pltpu.roll(tile, LEAF, 1)
        xdup[first] = jnp.where(low, tile, turned).astype(BF16)
        xdup[first + 1] = jnp.where(low, turned, tile).astype(BF16)

    def remote(src, dst, send, recv, to):
        return pltpu.make_async_remote_copy(
            src_ref=src, dst_ref=dst, send_sem=send, recv_sem=recv, device_id=to, device_id_type=MESH
        )

    def all_sum(at, rows):
        spot = lane - iota((count, LANES), 0)
        spread_out = jnp.zeros((count, LANES), F32)
        for k, acc in enumerate(rows):
            spread_out = jnp.where(spot == k * count, jnp.sum(acc, axis=1, keepdims=True), spread_out)
        line = jnp.sum(spread_out, axis=0, keepdims=True)
        part[at] = line
        sums[at, 0] = line

        def copy(s):
            return remote(part.at[at], sums.at[at, s], sum_s.at[at, s], sum_r.at[at, s], any_id(s))

        def start(s, carry):
            copy(s).start()
            return carry

        def wait(s, carry):
            copy(s).wait()
            return carry

        lax.fori_loop(1, total, start, 0)
        lax.fori_loop(1, total, wait, 0)
        parts = [sums[at, lax.rem(me + total - d, total)] for d in range(total)]
        while len(parts) > 1:
            parts = [parts[i] + parts[i + 1] for i in range(0, len(parts), 2)]
        line = parts[0]
        return [
            jnp.sum(jnp.where(spot == k * count, line, 0.0), axis=1, keepdims=True) for k in range(len(rows))
        ]

    def operator(at, x, w, others):
        h_low = remote(xbf.at[:, width - edge:width], halo.at[at, 0], halo_s.at[at, 0], halo_r.at[at, 0], after_id)
        h_high = remote(xbf.at[:, 0:edge], halo.at[at, 1], halo_s.at[at, 1], halo_r.at[at, 1], before_id)
        h_low.start()
        h_high.start()
        tiles = slots // QUAD
        for g4 in range(leaves // QUAD):
            z = dot(xbf[:, g4 * 256:(g4 + 1) * 256], v_big[g4 * 256:(g4 + 1) * 256, :])
            zbuf[g4 // tiles, :, g4 % tiles * LANES:(g4 % tiles + 1) * LANES] = z.astype(BF16)
        z_copies = []
        for s in range(1, n_col):
            z_copies.append(
                remote(zbuf.at[lax.rem(col + s, n_col)], zrecv.at[at, s], z_s.at[at, s], z_r.at[at, s], col_id(s))
            )
            z_copies[-1].start()
        zrecv[at, 0] = zbuf[col]
        if at == 0:
            prepare_near()
        h_low.wait()
        h_high.wait()
        for side, beyond, first in ((0, me == 0, 0), (1, me == total - 1, leaves + HALO)):
            for k in range(HALO // 2):
                tile = halo[at, side, :, k * LANES:(k + 1) * LANES].astype(F32)
                spread(jnp.where(beyond, 0.0, tile), first + 2 * k)

        def near(b, carry):
            for pair in range(4):
                outs = []
                for k in range(2):
                    leaf = b * 8 + pair * 2 + k
                    picked = [xdup[leaf + HALO + offs[leaf, n]] for n in range(nnear)]
                    left = jnp.concatenate(
                        [jnp.where(low, picked[2 * m], picked[2 * m + 1]) for m in range(nnear // 2)], axis=1
                    )
                    outs.append(
                        lax.dot_general(
                            left, near_w[lanes_at(leaf, LEAF), :], (((1,), (1,)), ((), ())),
                            preferred_element_type=F32,
                        )
                    )
                where = lanes_at(b * 4 + pair, LANES)
                w[:, where] = x[:, where] + jnp.concatenate(outs, axis=1)
            return carry

        steps = leaves // 8
        lax.fori_loop(0, steps // 2, near, 0)
        for copy in z_copies:
            copy.wait()
        if at == 0:
            loads["mixc"].wait()
        for jt in range(tiles):
            lefts = [[] for _ in range(QUAD)]
            for cq in range(n_col // QUAD):
                got = regroup(
                    [
                        zrecv[at, lax.rem(col + n_col - (cq * QUAD + c4), n_col), :, jt * LANES:(jt + 1) * LANES].astype(F32)
                        for c4 in range(QUAD)
                    ],
                    group,
                )
                for j4 in range(QUAD):
                    lefts[j4].append(got[j4].astype(BF16))
            for j4 in range(QUAD):
                j = jt * QUAD + j4
                first = dot(jnp.concatenate(lefts[j4], axis=1), mixc[j])
                tbuf[j // sub, j % sub] = first.astype(BF16)
        t_copies = []
        for s in range(1, n_row):
            t_copies.append(
                remote(tbuf.at[lax.rem(row + s, n_row)], trecv.at[at, s], t_s.at[at, s], t_r.at[at, s], row_id(s))
            )
            t_copies[-1].start()
        trecv[at, 0] = tbuf[row]
        if at == 0:
            prepare_u()
        lax.fori_loop(steps // 2, steps, near, 0)
        for copy in t_copies:
            copy.wait()
        if at == 0:
            loads["mixr"].wait()
        accs = [jnp.zeros((count, LANES), F32) for _ in range(len(others) + 1)]
        for i in range(sub):
            for pq in range(n_col // QUAD):
                lefts = [[] for _ in range(QUAD)]
                for rq in range(n_row // QUAD):
                    got = regroup(
                        [
                            trecv[at, lax.rem(row + n_row - (rq * QUAD + r4), n_row), i, :, pq * LANES:(pq + 1) * LANES].astype(F32)
                            for r4 in range(QUAD)
                        ],
                        group,
                    )
                    for p4 in range(QUAD):
                        lefts[p4].append(got[p4].astype(BF16))
                for p4 in range(QUAD):
                    p = pq * QUAD + p4
                    second = dot(jnp.concatenate(lefts[p4], axis=1), mixr[i, p]).astype(BF16)
                    for tt in range(n_row // QUAD):
                        at4 = (i * n_col + p) * (n_row // QUAD) + tt
                        far = dot(second[:, tt * LANES:(tt + 1) * LANES], u_big[at4 * LANES:(at4 + 1) * LANES, :])
                        for k in range(2):
                            where = slice(at4 * 256 + k * LANES, at4 * 256 + (k + 1) * LANES)
                            image = w[:, where] + far[:, k * LANES:(k + 1) * LANES]
                            w[:, where] = image
                            for m, other in enumerate(others):
                                accs[m] = accs[m] + other[:, where] * image
                            accs[-1] = accs[-1] + image * image
        return accs

    prepare_v()
    loads["rhs"].wait()

    def start_tile(t, acc):
        where = lanes_at(t, LANES)
        tile = rhs[:, where]
        xbf[:, where] = tile.astype(BF16)
        spread(tile, HALO + 2 * t)
        return acc + tile * tile

    norm = lax.fori_loop(0, width // LANES, start_tile, jnp.zeros((count, LANES), F32))
    pl.semaphore_wait(barrier, total - 1)
    first = operator(0, rhs, w_one, (rhs,))
    norm_sq, cross, image_sq = all_sum(0, [norm] + first)
    beta = jnp.sqrt(norm_sq)
    h11 = cross / norm_sq
    h21 = jnp.sqrt(image_sq / norm_sq - h11 * h11)
    scale = 1.0 / (beta * h21)

    def second_tile(t, carry):
        where = lanes_at(t, LANES)
        tile = (w_one[:, where] - h11 * rhs[:, where]) * scale
        q_two[:, where] = tile
        xbf[:, where] = tile.astype(BF16)
        spread(tile, HALO + 2 * t)
        return carry

    lax.fori_loop(0, width // LANES, second_tile, 0)
    second = operator(1, q_two, w_two, (rhs, q_two))
    with_first, h22, image_sq = all_sum(1, second)
    h12 = with_first / beta
    h32 = jnp.sqrt(image_sq - (h12 * h12 + h22 * h22))
    m11 = h11 * h11 + h21 * h21
    m12 = h11 * h12 + h21 * h22
    m22 = h12 * h12 + h22 * h22 + h32 * h32
    det = m11 * m22 - m12 * m12
    y1 = (m22 * h11 - m12 * h12) / det
    y2 = beta * (m11 * h12 - m12 * h11) / det

    def last_tile(t, carry):
        where = lanes_at(t, LANES)
        sol[:, where] = y1 * rhs[:, where] + y2 * q_two[:, where]
        res[:, where] = rhs[:, where] - y1 * w_one[:, where] - y2 * w_two[:, where]
        return carry

    lax.fori_loop(0, width // LANES, last_tile, 0)


def body(rhs, near_blocks, near_offsets, v_factor, mix_col, mix_row, u_factor):
    n_row = lax.axis_size("row")
    n_col = lax.axis_size("col")
    count, width = rhs.shape
    leaves, nnear = near_offsets.shape
    pieces = near_blocks.shape[2] // LANES
    near_rows = (
        near_blocks.reshape(leaves, nnear, pieces, LANES).transpose(0, 2, 1, 3).reshape(leaves * pieces * nnear, LANES)
    )
    mixc = mix_col[0]
    slots = leaves // n_col
    sub = slots // n_row
    total = n_row * n_col
    operands = (rhs, near_rows, v_factor, mixc, mix_row, u_factor)
    vmem = pltpu.VMEM
    dma = pltpu.SemaphoreType.DMA
    field = vmem((count, width), F32)
    hbm_spec = pl.BlockSpec(memory_space=pltpu.HBM)
    return pl.pallas_call(
        kernel,
        out_shape=(jax.ShapeDtypeStruct((count, width), F32),) * 2,
        in_specs=[pl.BlockSpec(memory_space=pltpu.SMEM)] + [hbm_spec] * 6,
        out_specs=(pl.BlockSpec(memory_space=pltpu.VMEM),) * 2,
        scratch_shapes=[
            field,
            vmem(near_rows.shape, BF16),
            vmem(v_factor.shape, BF16),
            vmem(mixc.shape, BF16),
            vmem(mix_row.shape, BF16),
            vmem(u_factor.shape, BF16),
            vmem((leaves * LEAF, nnear * LEAF), BF16),
            vmem((leaves * LEAF, LANES), BF16),
            vmem((leaves * RANK, 2 * LANES), BF16),
            vmem((nnear * LEAF, pieces * nnear), BF16),
            vmem((16 * LEAF, 256), BF16),
            vmem((16 * RANK, 256), BF16),
            vmem((count, width), BF16),
            vmem((leaves + 2 * HALO, count, LANES), BF16),
            field,
            field,
            field,
            vmem((n_col, count, slots * RANK), BF16),
            vmem((2, n_col, count, slots * RANK), BF16),
            vmem((n_row, sub, count, n_col * RANK), BF16),
            vmem((2, n_row, sub, count, n_col * RANK), BF16),
            vmem((2, 2, count, HALO * LEAF), BF16),
            vmem((2, 1, LANES), F32),
            vmem((2, total, 1, LANES), F32),
            dma((6,)),
            dma((2, 2)),
            dma((2, 2)),
            dma((2, n_col)),
            dma((2, n_col)),
            dma((2, n_row)),
            dma((2, n_row)),
            dma((2, total)),
            dma((2, total)),
        ],
        compiler_params=pltpu.CompilerParams(
            collective_id=0, has_side_effects=True, vmem_limit_bytes=34 * 1024 * 1024
        ),
        name="gmres",
    )(near_offsets, *(pltpu.with_memory_space_constraint(a, pltpu.HBM) for a in operands))


def solution(mesh):
    in_specs = (
        P(None, ("row", "col")),
        P(("row", "col"), None, None),
        P(("row", "col"), None),
        P(("row", "col"), None),
        P("row", "col", None, None),
        P("row", "col", None, None),
        P(("row", "col"), None),
    )
    out_specs = (P(None, ("row", "col")), P(None, ("row", "col")))
    return jax.shard_map(body, mesh=mesh, in_specs=in_specs, out_specs=out_specs, check_vma=False)
```

profile of v0, /device:TPU:1, one launch (start us, length us, event | category | flops | bytes accessed | tf_op | source)
XLA Modules:
  0.0 83.5 jit_solution(6040552166161590988)
XLA Ops:
  0.6 0.8 copy.10.offs
  1.4 80.2 %gmres.1 = (f32[32,8192]{1,0:T(8,128)S(1)}, f32[32,8192]{1,0:T(8,128)S(1)}) custom-call(s32[128,4]{1,0:T(8,128)S(1)} %copy.10.offs, f32[32,8192]{1,0:T(8,128)} %rhs_h.1, bf16[16384,128]{1,0:T(8,128)(2,1)} %bitcast.6, bf16[128,2048]{1,0:T(8,128)(2,1)} %v_h.1, bf16[8,512,512]{2,1,0:T(8,128)(2,1)} %bitcast.7, bf16[1,16,256,256]{3,2,1,0:T(8,128)(2,1)} %mixr_h.1, ...), custom_call_target="tpu_custom_call" | custom-call | tf_op jit(solution)/shard_map/gmres/pallas_call | solution.py:402
  81.6 1.0 %copy.13 = f32[32,8192]{1,0:T(8,128)} copy(f32[32,8192]{1,0:T(8,128)S(1)} %get-tuple-element.4) | data formatting | bytes 2097152
  82.6 1.0 %copy.14 = f32[32,8192]{1,0:T(8,128)} copy(f32[32,8192]{1,0:T(8,128)S(1)} %get-tuple-element.5) | data formatting | bytes 2097152
where the time goes:
time: 83.7 us; the launch traced here: 83.5 us
  Pallas kernels  80.2 us (96%)
  local copies, waits for them, and re-layouts  2.73 us (3%)
    pallas_call x1, Pallas kernels, body(): pl.pallas_call(kernel, out_shape=(jax.ShapeDtypeStruct((count, width), F3...  80.2 us
    unnamed x3, local copies, waits for them, and re-layouts  2.73 us

commit v1 on v0

v1 whole, which is shorter than its diff:
```python
import jax
import jax.numpy as jnp
from jax import lax
from jax.experimental import pallas as pl
from jax.experimental.pallas import tpu as pltpu
from jax.sharding import PartitionSpec as P

LEAF = 64
RANK = 32
HALO = 4
LANES = 128
QUAD = LANES // RANK
PAIRS_STEP = 16
BF16 = jnp.bfloat16
F32 = jnp.float32
MESH = pl.DeviceIdType.MESH


def iota(shape, dim):
    return lax.broadcasted_iota(jnp.int32, shape, dim)


def dot(a, b):
    return jnp.dot(a, b, preferred_element_type=F32)


def dot_t(a, b):
    return lax.dot_general(a, b, (((1,), (1,)), ((), ())), preferred_element_type=F32)


def lanes_at(index, width):
    return pl.ds(pl.multiple_of(index * width, width), width)


def regroup(tiles, group):
    out = []
    for j in range(QUAD):
        made = None
        for c in range(QUAD):
            shift = (c - j) * RANK % LANES
            moved = pltpu.roll(tiles[c], shift, 1) if shift else tiles[c]
            made = moved if made is None else jnp.where(group == c, moved, made)
        out.append(made)
    return out


def tree(parts):
    while len(parts) > 1:
        parts = [parts[i] + parts[i + 1] for i in range(0, len(parts), 2)]
    return parts[0]


def kernel(
    offs_h, rhs_h, near_h, v_h, mixc_h, mixr_h, u_h, rhs, x, y, coef,
    offs, near_raw, v_raw, mixc, mixr, u_raw,
    near_w, v_big, u_big, pick_near, pick_v, pick_u,
    xbf, xdup, nacc, left_r,
    zbuf, zrecv, tbuf, trecv, halo, part, sums,
    load_sem, halo_s, halo_r, z_s, z_r, t_s, t_r, sum_s, sum_r,
):
    n_row = lax.axis_size("row")
    n_col = lax.axis_size("col")
    total = n_row * n_col
    row = lax.axis_index("row")
    col = lax.axis_index("col")
    me = row * n_col + col
    count, width = rhs.shape
    leaves = width // LEAF
    nnear = offs.shape[0]
    slots = leaves // n_col
    tiles = slots // QUAD
    edge = HALO * LEAF

    loads = {}
    for at, (name, src, dst) in enumerate(
        (("v", v_h, v_raw), ("rhs", rhs_h, rhs), ("offs", offs_h, offs), ("near", near_h, near_raw),
         ("mixc", mixc_h, mixc), ("u", u_h, u_raw), ("mixr", mixr_h, mixr))
    ):
        loads[name] = pltpu.make_async_copy(src, dst, load_sem.at[at])
        if name in ("v", "rhs", "offs"):
            loads[name].start()

    barrier = pltpu.get_barrier_semaphore()
    before = lax.rem(me + total - 1, total)
    after = lax.rem(me + 1, total)
    before_id = (before // n_col, lax.rem(before, n_col))
    after_id = (after // n_col, lax.rem(after, n_col))
    rows = [row] + [lax.rem(row + i, n_row) for i in range(1, n_row)]
    cols = [col] + [lax.rem(col + i, n_col) for i in range(1, n_col)]
    others = [(i, j) for i in range(n_row) for j in range(n_col) if i or j]

    for i, j in others:
        pl.semaphore_signal(barrier, inc=1, device_id=(rows[i], cols[j]), device_id_type=MESH)

    lane = iota((count, LANES), 1)
    low = lane < LEAF
    group = lane // RANK

    shape = (256, 256)
    r = iota(shape, 0)
    c = iota(shape, 1)
    same = (c % 16 == r // 16) & (c // 16 % 4 == r // 4 % 4)
    pick_v[...] = jnp.where(same & (c // 64 == (r // 16 + 4 - r % 4) % 4), 1.0, 0.0).astype(BF16)
    same = (c % 16 == r // 16) & (c // 16 % 8 == r // 2 % 8)
    pick_u[...] = jnp.where(same & (c // 128 == (r // 16 + r) % 2), 1.0, 0.0).astype(BF16)
    shape = (LANES, 256)
    r = iota(shape, 0)
    c = iota(shape, 1)
    b = c % nnear
    same = (c % LANES // nnear == r % LEAF // 2) & (b // 2 == r // LEAF)
    pick_near[...] = jnp.where(same & (c // LANES == (r + b) % 2), 1.0, 0.0).astype(BF16)

    def turned(tile, shift):
        return pltpu.roll(tile, shift, 1) if shift else tile

    def prepare_v():
        lane16 = iota((16, LANES), 1) // RANK
        place = lane16 == iota((16, LANES), 0) % QUAD
        for b in range(leaves // 32):
            sides = []
            for h in range(2):
                base = b * 32 + h * 16
                raw = [v_raw[base:base + 16, t * LANES:(t + 1) * LANES].astype(F32) for t in range(16)]
                sides.append(
                    [[jnp.where(place, turned(a, d * RANK), 0.0).astype(BF16) for a in raw] for d in range(4)]
                )
            for q in range(4):
                both = jnp.concatenate(
                    [
                        jnp.concatenate([s[d][4 * q + t] for d in range(4) for t in range(4)], axis=0)
                        for s in sides
                    ],
                    axis=1,
                )
                made = dot(pick_v[...], both)
                for h in range(2):
                    for i in range(16):
                        at = (b * 32 + h * 16 + i) * LEAF + q * 16
                        v_big[at:at + 16, :] = made[i * 16:(i + 1) * 16, h * LANES:(h + 1) * LANES].astype(BF16)

    def prepare_u():
        lane16 = iota((16, LANES), 1) // LEAF
        place = lane16 == iota((16, LANES), 0) % 2
        blank = jnp.zeros((16, LANES), BF16)
        for b in range(leaves // 32):
            sides = []
            for h in range(2):
                base = b * 32 + h * 16
                raw = [u_raw[base:base + 16, t * LANES:(t + 1) * LANES].astype(F32) for t in range(16)]
                sides.append(
                    [[jnp.where(place, turned(a, d * LEAF), 0.0).astype(BF16) for a in raw] for d in range(2)]
                )
            for q in range(2):
                both = jnp.concatenate(
                    [
                        jnp.concatenate([s[d][8 * q + t] for d in range(2) for t in range(8)], axis=0)
                        for s in sides
                    ],
                    axis=1,
                )
                made = dot(pick_u[...], both)
                for h in range(2):
                    for i in range(16):
                        at = (b * 32 + h * 16 + i) * RANK + q * 16
                        side = i % QUAD // 2
                        tile = made[i * 16:(i + 1) * 16, h * LANES:(h + 1) * LANES].astype(BF16)
                        u_big[at:at + 16, side * LANES:(side + 1) * LANES] = tile
                        u_big[at:at + 16, (1 - side) * LANES:(2 - side) * LANES] = blank

    def prepare_near():
        size = nnear * LEAF // 2
        keep = (iota((size, LANES), 1) // LEAF) == iota((size, LANES), 0) % 2

        def block(b, carry):
            for k in range(PAIRS_STEP):
                pair = b * PAIRS_STEP + k
                sides = []
                for h in range(2):
                    raw = near_raw[lanes_at(pair * 2 + h, size), :].astype(F32)
                    sides.append(
                        jnp.concatenate(
                            [
                                jnp.where(keep, raw, 0.0).astype(BF16),
                                jnp.where(keep, pltpu.roll(raw, LEAF, 1), 0.0).astype(BF16),
                            ],
                            axis=0,
                        )
                    )
                made = dot(pick_near[...], jnp.concatenate(sides, axis=1))
                for h in range(2):
                    for m in range(nnear // 2):
                        near_w[lanes_at(pair * 2 + h, LEAF), m * LANES:(m + 1) * LANES] = made[
                            m * LEAF:(m + 1) * LEAF, h * LANES:(h + 1) * LANES
                        ].astype(BF16)
            return carry

        lax.fori_loop(0, leaves // 2 // PAIRS_STEP, block, 0)

    def spread(tile, first):
        swapped = pltpu.roll(tile, LEAF, 1)
        xdup[first] = jnp.where(low, tile, swapped).astype(BF16)
        xdup[first + 1] = jnp.where(low, swapped, tile).astype(BF16)

    def remote(src, dst, send, recv, to):
        return pltpu.make_async_remote_copy(
            src_ref=src, dst_ref=dst, send_sem=send, recv_sem=recv, device_id=to, device_id_type=MESH
        )

    def sum_copy(at, i, j):
        s = i * n_col + j
        return remote(part.at[at], sums.at[at, s], sum_s.at[at], sum_r.at[at], (rows[i], cols[j]))

    def sum_start(at, accs):
        spot = lane - iota((count, LANES), 0)
        spread_out = jnp.zeros((count, LANES), F32)
        for k, acc in enumerate(accs):
            spread_out = jnp.where(spot == k * count, jnp.sum(acc, axis=1, keepdims=True), spread_out)
        line = jnp.sum(spread_out, axis=0, keepdims=True)
        part[at] = line
        sums[at, 0] = line
        for i, j in others:
            sum_copy(at, i, j).start()

    def sum_finish(at, many):
        everything = remote(
            sums.at[at, 1:total], sums.at[at, 1:total], sum_s.at[at], sum_r.at[at], (rows[0], cols[1])
        )
        everything.wait_send()
        everything.wait_recv()
        line = tree([sums[at, d] for d in range(total)])
        spot = lane - iota((count, LANES), 0)
        return [jnp.sum(jnp.where(spot == k * count, line, 0.0), axis=1, keepdims=True) for k in range(many)]

    def z_dot(g4, at4):
        z = dot(xbf[:, lanes_at(at4, 256)], v_big[lanes_at(at4, 256), :])
        g, side = g4
        zbuf[g, :, side * LANES:(side + 1) * LANES] = z.astype(BF16)

    def z_copy(at, s):
        return remote(zbuf.at[cols[s]], zrecv.at[at, s], z_s.at[at, s], z_r.at[at, s], (row, cols[s]))

    def t_copy(at, s):
        return remote(tbuf.at[rows[s]], trecv.at[at, s], t_s.at[at, s], t_r.at[at, s], (rows[s], col))

    def halo_copy(at, side):
        src = xbf.at[:, width - edge:width] if side == 0 else xbf.at[:, 0:edge]
        return remote(src, halo.at[at, side], halo_s.at[at, side], halo_r.at[at, side], (after_id, before_id)[side])

    def near(b, carry):
        for k in range(PAIRS_STEP):
            pair = b * PAIRS_STEP + k
            lefts = []
            for h in range(2):
                leaf = pair * 2 + h
                picked = [xdup[leaf + HALO]] + [xdup[leaf + HALO + offs[n, leaf]] for n in range(1, nnear)]
                lefts.append(
                    jnp.concatenate(
                        [jnp.where(low, picked[2 * m], picked[2 * m + 1]) for m in range(nnear // 2)], axis=1
                    )
                )
            both = dot_t(jnp.concatenate(lefts, axis=0), near_w[lanes_at(pair, 2 * LEAF), :])
            nacc[:, lanes_at(pair, LANES)] = jnp.where(low, both[:count], both[count:])
        return carry

    steps = leaves // 2 // PAIRS_STEP

    def operator(at, out, add, dots, follow):
        for s in range(1, n_col):
            z_copy(at, s).start()
        zrecv[at, 0] = zbuf[col]
        if at == 0:
            loads["near"].wait()
            prepare_near()
            loads["offs"].wait()
        for side in range(2):
            halo_copy(at, side).wait()
        for side, beyond, first in ((0, me == 0, 0), (1, me == total - 1, leaves + HALO)):
            for k in range(HALO // 2):
                tile = halo[at, side, :, k * LANES:(k + 1) * LANES].astype(F32)
                spread(jnp.where(beyond, 0.0, tile), first + 2 * k)
        split = steps // 4 if at == 0 else steps // 2
        lax.fori_loop(0, split, near, 0)
        for s in range(1, n_col):
            z_copy(at, s).wait()
        if at == 0:
            loads["mixc"].wait()
        for jt in range(tiles):
            lefts = [[] for _ in range(QUAD)]
            for cq in range(n_col // QUAD):
                got = regroup(
                    [
                        zrecv[at, lax.rem(col + n_col - (cq * QUAD + c4), n_col), :, jt * LANES:(jt + 1) * LANES].astype(F32)
                        for c4 in range(QUAD)
                    ],
                    group,
                )
                for j4 in range(QUAD):
                    lefts[j4].append(got[j4].astype(BF16))
            for j4 in range(QUAD):
                j = jt * QUAD + j4
                tbuf[j] = dot(jnp.concatenate(lefts[j4], axis=1), mixc[j]).astype(BF16)
        for s in range(1, n_row):
            t_copy(at, s).start()
        trecv[at, 0] = tbuf[row]
        if at == 0:
            loads["u"].wait()
            prepare_u()
        lax.fori_loop(split, steps, near, 0)
        for s in range(1, n_row):
            t_copy(at, s).wait()
        if at == 0:
            loads["mixr"].wait()
        for pq in range(n_col // QUAD):
            for rq in range(n_row // QUAD):
                got = regroup(
                    [
                        trecv[at, lax.rem(row + n_row - (rq * QUAD + r4), n_row), :, pq * LANES:(pq + 1) * LANES].astype(F32)
                        for r4 in range(QUAD)
                    ],
                    group,
                )
                for p4 in range(QUAD):
                    left_r[pq * QUAD + p4, :, rq * LANES:(rq + 1) * LANES] = got[p4].astype(BF16)
        accs = [jnp.zeros((count, LANES), F32) for _ in range(len(dots) + 1)]
        for s in range(1, n_col + 1):
            p = cols[s % n_col]
            second = dot(left_r[p], mixr[p]).astype(BF16)
            for tt in range(n_row // QUAD):
                at4 = p * (n_row // QUAD) + tt
                far = dot(second[:, tt * LANES:(tt + 1) * LANES], u_big[lanes_at(at4, LANES), :])
                for k in range(2):
                    where = lanes_at(at4 * 2 + k, LANES)
                    image = nacc[:, where] + far[:, k * LANES:(k + 1) * LANES]
                    if add is not None:
                        image = add[:, where] + image
                    out[:, where] = image
                    for m, other in enumerate(dots):
                        accs[m] = accs[m] + other[:, where] * image
                    accs[-1] = accs[-1] + image * image
                    if follow:
                        xbf[:, where] = image.astype(BF16)
                        spread(image, HALO + (at4 * 2 + k) * 2)
                if follow:
                    z_dot((p, tt), at4)
        return accs

    loads["v"].wait()
    for name in ("near", "mixc", "u", "mixr"):
        loads[name].start()
    prepare_v()
    loads["rhs"].wait()
    norm = jnp.zeros((count, LANES), F32)
    for t in range(width // LANES):
        tile = rhs[:, t * LANES:(t + 1) * LANES]
        xbf[:, t * LANES:(t + 1) * LANES] = tile.astype(BF16)
        spread(tile, HALO + 2 * t)
        norm = norm + tile * tile
        if t % 2:
            g4 = t // 2
            z_dot((g4 // tiles, g4 % tiles), g4)
    pl.semaphore_wait(barrier, total - 1)
    for side in range(2):
        halo_copy(0, side).start()
    first = operator(0, x, None, (rhs,), True)
    for side in range(2):
        halo_copy(1, side).start()
    sum_start(0, [norm] + first)
    second = operator(1, y, x, (rhs, x), False)
    sum_start(1, second)
    rr, rx, xx = sum_finish(0, 3)
    ry, xy, yy = sum_finish(1, 3)

    beta = jnp.sqrt(rr)
    d = rx / rr
    h11 = 1.0 + d
    rho_sq = xx - d * rx
    rho = jnp.sqrt(rho_sq)
    h21 = rho / beta
    h12 = (ry - d * (rr + rx)) / (beta * rho)
    across = xy - d * ry
    h22 = across / rho_sq - d
    h32 = jnp.sqrt((yy - ry * ry / rr - across * across / rho_sq) / rho_sq)
    m11 = h11 * h11 + h21 * h21
    m12 = h11 * h12 + h21 * h22
    m22 = h12 * h12 + h22 * h22 + h32 * h32
    det = m11 * m22 - m12 * m12
    y1 = (m22 * h11 - m12 * h12) / det
    y2 = beta * (m11 * h12 - m12 * h11) / det
    on_x = y2 / rho
    on_r = y1 - on_x * d
    coef[0] = jnp.broadcast_to(on_r, (count, LANES))
    coef[1] = jnp.broadcast_to(on_x, (count, LANES))


CHUNKS = 4


def finish(coef, rhs, x, y, sol_h, res_h, sol, res, sem):
    count, width = rhs.shape
    on_r = coef[0]
    on_x = coef[1]
    size = width // CHUNKS
    copies = []
    for c in range(CHUNKS):
        for t in range(size // LANES):
            where = slice(c * size + t * LANES, c * size + (t + 1) * LANES)
            r_tile = rhs[:, where]
            x_tile = x[:, where]
            sol[:, where] = on_r * r_tile + on_x * x_tile
            res[:, where] = r_tile - on_r * (r_tile + x_tile) - on_x * y[:, where]
        span = slice(c * size, (c + 1) * size)
        for k, (src, dst) in enumerate(((sol, sol_h), (res, res_h))):
            copies.append(pltpu.make_async_copy(src.at[:, span], dst.at[:, span], sem.at[c, k]))
            copies[-1].start()
    for copy in copies:
        copy.wait()


def body(rhs, near_blocks, near_offsets, v_factor, mix_col, mix_row, u_factor):
    n_row = lax.axis_size("row")
    n_col = lax.axis_size("col")
    count, width = rhs.shape
    leaves, nnear = near_offsets.shape
    pieces = near_blocks.shape[2] // LANES
    near_rows = (
        near_blocks.reshape(leaves, nnear, pieces, LANES).transpose(0, 2, 1, 3).reshape(leaves * pieces * nnear, LANES)
    )
    mixc = mix_col[0]
    mixr = mix_row[0]
    slots = leaves // n_col
    total = n_row * n_col
    operands = (near_offsets.T, rhs, near_rows, v_factor, mixc, mixr, u_factor)
    vmem = pltpu.VMEM
    dma = pltpu.SemaphoreType.DMA
    field = jax.ShapeDtypeStruct((count, width), F32)
    hbm_spec = pl.BlockSpec(memory_space=pltpu.HBM)
    vmem_spec = pl.BlockSpec(memory_space=pltpu.VMEM)
    rhs_v, x, y, coef = pl.pallas_call(
        kernel,
        out_shape=(field, field, field, jax.ShapeDtypeStruct((2, count, LANES), F32)),
        in_specs=[hbm_spec] * 7,
        out_specs=(vmem_spec,) * 4,
        scratch_shapes=[
            pltpu.SMEM((nnear, leaves), jnp.int32),
            vmem(near_rows.shape, BF16),
            vmem(v_factor.shape, BF16),
            vmem(mixc.shape, BF16),
            vmem(mixr.shape, BF16),
            vmem(u_factor.shape, BF16),
            vmem((leaves * LEAF, nnear * LEAF), BF16),
            vmem((leaves * LEAF, LANES), BF16),
            vmem((leaves * RANK, 2 * LANES), BF16),
            vmem((LANES, 256), BF16),
            vmem((256, 256), BF16),
            vmem((256, 256), BF16),
            vmem((count, width), BF16),
            vmem((leaves + 2 * HALO, count, LANES), BF16),
            vmem((count, width), F32),
            vmem((n_col, count, n_row * RANK), BF16),
            vmem((n_col, count, slots * RANK), BF16),
            vmem((2, n_col, count, slots * RANK), BF16),
            vmem((n_row, count, n_col * RANK), BF16),
            vmem((2, n_row, count, n_col * RANK), BF16),
            vmem((2, 2, count, HALO * LEAF), BF16),
            vmem((2, 1, LANES), F32),
            vmem((2, total, 1, LANES), F32),
            dma((7,)),
            dma((2, 2)),
            dma((2, 2)),
            dma((2, n_col)),
            dma((2, n_col)),
            dma((2, n_row)),
            dma((2, n_row)),
            dma((2,)),
            dma((2,)),
        ],
        compiler_params=pltpu.CompilerParams(
            collective_id=0, has_side_effects=True, vmem_limit_bytes=34 * 1024 * 1024
        ),
        name="gmres",
    )(*(pltpu.with_memory_space_constraint(a, pltpu.HBM) for a in operands))
    return pl.pallas_call(
        finish,
        out_shape=(field, field),
        in_specs=[vmem_spec] * 4,
        out_specs=(hbm_spec,) * 2,
        scratch_shapes=[vmem((count, width), F32), vmem((count, width), F32), dma((CHUNKS, 2))],
        compiler_params=pltpu.CompilerParams(vmem_limit_bytes=16 * 1024 * 1024),
        name="combine",
    )(coef, rhs_v, x, y)


def solution(mesh):
    in_specs = (
        P(None, ("row", "col")),
        P(("row", "col"), None, None),
        P(("row", "col"), None),
        P(("row", "col"), None),
        P("row", "col", None, None),
        P("row", "col", None, None),
        P(("row", "col"), None),
    )
    out_specs = (P(None, ("row", "col")), P(None, ("row", "col")))
    return jax.shard_map(body, mesh=mesh, in_specs=in_specs, out_specs=out_specs, check_vma=False)
```

time: 83.7 us -> 49.2 us (0.59)
  Pallas kernels: 80.2 us -> 48.5 us
  local copies, waits for them, and re-layouts: 2.73 us -> 0 us
    pallas_call x1 -> x2, Pallas kernels: 80.2 us -> 48.5 us  [the longest x1 47 us: body(): pl.pallas_call(kernel, out_shape=(field, field, field, jax.ShapeDtypeStru...]
    unnamed x3 -> x0, local copies, waits for them, and re-layouts: 2.73 us -> none
where the time goes in v1:
time: 49.2 us; the launch traced here: 49.1 us
  Pallas kernels  48.5 us (99%)
  between operations  0.64 us (1%)
    pallas_call x1, Pallas kernels, body(): pl.pallas_call(kernel, out_shape=(field, field, field, jax.ShapeDtypeStru...  47 us
    pallas_call x1, Pallas kernels, body(): pl.pallas_call(finish, out_shape=(field, field), in_specs=[vmem_spec] * 4...  1.43 us

profile of v1, /device:TPU:1, one launch (start us, length us, event | category | flops | bytes accessed | tf_op | source)
XLA Modules:
  0.0 49.1 jit_solution(2602588907376917183)
XLA Ops:
  0.6 47.0 %gmres.1 = (f32[32,8192]{1,0:T(8,128)S(1)}, f32[32,8192]{1,0:T(8,128)S(1)}, f32[32,8192]{1,0:T(8,128)S(1)}, f32[2,32,128]{2,1,0:T(8,128)S(1)}) custom-call(s32[4,128]{1,0:T(4,128)} %bitcast.11, f32[32,8192]{1,0:T(8,128)} %rhs_h.1, bf16[16384,128]{1,0:T(8,128)(2,1)} %bitcast.8, bf16[128,2048]{1,0:T(8,128)(2,1)} %v_h.1, bf16[8,512,512]{2,1,0:T(8,128)(2,1)} %bitcast.9, ...), custom_call_target="tpu_custom_call" | custom-call | tf_op jit(solution)/shard_map/gmres/pallas_call | solution.py:438
  47.7 1.4 %combine.1 = (f32[32,8192]{1,0:T(8,128)}, f32[32,8192]{1,0:T(8,128)}) custom-call(f32[2,32,128]{2,1,0:T(8,128)S(1)} %get-tuple-element.6.coef, f32[32,8192]{1,0:T(8,128)S(1)} %get-tuple-element.7.rhs, f32[32,8192]{1,0:T(8,128)S(1)} %get-tuple-element.8.x, f32[32,8192]{1,0:T(8,128)S(1)} %get-tuple-element.9.y), custom_call_target="tpu_custom_call" | custom-call | tf_op jit(solution)/shard_map/combine/pallas_call | solution.py:482

commit v2 on v1

--- a/solution.py
+++ b/solution.py
@@ -11,6 +11,9 @@
 LANES = 128
 QUAD = LANES // RANK
 PAIRS_STEP = 16
+T_GROUP = 4
+Z_GROUP = 16
+RING = 4
 BF16 = jnp.bfloat16
 F32 = jnp.float32
 MESH = pl.DeviceIdType.MESH
@@ -54,9 +57,9 @@
     offs_h, rhs_h, near_h, v_h, mixc_h, mixr_h, u_h, rhs, x, y, coef,
     offs, near_raw, v_raw, mixc, mixr, u_raw,
     near_w, v_big, u_big, pick_near, pick_v, pick_u,
-    xbf, xdup, nacc, left_r,
-    zbuf, zrecv, tbuf, trecv, halo, part, sums,
-    load_sem, halo_s, halo_r, z_s, z_r, t_s, t_r, sum_s, sum_r,
+    rim, xdup, nacc, left_c, left_r,
+    zbuf, zrecv, tbuf, trecv, halo, part, early, sums,
+    load_sem, halo_s, halo_r, z_s, z_r, t_s, t_r, early_s, early_r, sum_s, sum_r,
 ):
     n_row = lax.axis_size("row")
     n_col = lax.axis_size("col")
@@ -69,7 +72,6 @@
     nnear = offs.shape[0]
     slots = leaves // n_col
     tiles = slots // QUAD
-    edge = HALO * LEAF
 
     loads = {}
     for at, (name, src, dst) in enumerate(
@@ -85,12 +87,37 @@
     after = lax.rem(me + 1, total)
     before_id = (before // n_col, lax.rem(before, n_col))
     after_id = (after // n_col, lax.rem(after, n_col))
-    rows = [row] + [lax.rem(row + i, n_row) for i in range(1, n_row)]
-    cols = [col] + [lax.rem(col + i, n_col) for i in range(1, n_col)]
+    cores = n_row // RING
+    place_x, place_core = row // cores, lax.rem(row, cores)
+    place_z, place_y = col // RING, lax.rem(col, RING)
+
+    def turn(base, by, size):
+        return lax.rem(base + by, size) if by else base
+
+    def away(by):
+        return min(by, RING - by)
+
+    rows = [turn(place_x, i // cores, RING) * cores + turn(place_core, i % cores, cores) for i in range(n_row)]
+    cols = [turn(place_z, j // RING, RING) * RING + turn(place_y, j % RING, RING) for j in range(n_col)]
+
+    def row_slot(r):
+        dx = lax.rem(place_x + RING - r // cores, RING)
+        return dx * cores + lax.rem(place_core + cores - r % cores, cores)
+
+    def col_slot(c):
+        dz = lax.rem(place_z + RING - c // RING, RING)
+        return dz * RING + lax.rem(place_y + RING - c % RING, RING)
+
+    row_far = [2 * away(i // cores) + i % cores for i in range(n_row)]
+    col_far = [2 * (away(j // RING) + away(j % RING)) for j in range(n_col)]
+    row_order = sorted(range(1, n_row), key=lambda i: -row_far[i])
+    col_order = sorted(range(1, n_col), key=lambda j: -col_far[j])
     others = [(i, j) for i in range(n_row) for j in range(n_col) if i or j]
-
-    for i, j in others:
-        pl.semaphore_signal(barrier, inc=1, device_id=(rows[i], cols[j]), device_id_type=MESH)
+    others.sort(key=lambda p: -(row_far[p[0]] + col_far[p[1]]))
+
+    greeted = [(row, cols[j]) for j in col_order] + [after_id, before_id] + [(rows[i], col) for i in row_order]
+    for peer in greeted:
+        pl.semaphore_signal(barrier, inc=1, device_id=peer, device_id_type=MESH)
 
     lane = iota((count, LANES), 1)
     low = lane < LEAF
@@ -206,35 +233,46 @@
             src_ref=src, dst_ref=dst, send_sem=send, recv_sem=recv, device_id=to, device_id_type=MESH
         )
 
-    def sum_copy(at, i, j):
-        s = i * n_col + j
-        return remote(part.at[at], sums.at[at, s], sum_s.at[at], sum_r.at[at], (rows[i], cols[j]))
-
-    def sum_start(at, accs):
+    def line_of(accs):
         spot = lane - iota((count, LANES), 0)
         spread_out = jnp.zeros((count, LANES), F32)
         for k, acc in enumerate(accs):
             spread_out = jnp.where(spot == k * count, jnp.sum(acc, axis=1, keepdims=True), spread_out)
-        line = jnp.sum(spread_out, axis=0, keepdims=True)
+        return jnp.sum(spread_out, axis=0, keepdims=True)
+
+    def columns_of(line, many):
+        spot = lane - iota((count, LANES), 0)
+        return [jnp.sum(jnp.where(spot == k * count, line, 0.0), axis=1, keepdims=True) for k in range(many)]
+
+    def group_copy(at, s):
+        to = (rows[s], col) if at == 0 else (row, cols[s])
+        return remote(part.at[at], early.at[at, s], early_s.at[at, s], early_r.at[at, s], to)
+
+    def group_start(at, line):
         part[at] = line
-        sums[at, 0] = line
+        early[at, 0] = line
+        for s in (row_order, col_order)[at]:
+            group_copy(at, s).start()
+
+    def group_finish(at):
+        for s in (row_order, col_order)[at]:
+            group_copy(at, s).wait()
+        return tree([early[at, d] for d in range((n_row, n_col)[at])])
+
+    def sum_start(line):
+        part[2] = line
+        sums[0] = line
         for i, j in others:
-            sum_copy(at, i, j).start()
-
-    def sum_finish(at, many):
-        everything = remote(
-            sums.at[at, 1:total], sums.at[at, 1:total], sum_s.at[at], sum_r.at[at], (rows[0], cols[1])
-        )
+            remote(part.at[2], sums.at[i * n_col + j], sum_s, sum_r, (rows[i], cols[j])).start()
+
+    def sum_finish():
+        everything = remote(sums.at[1:total], sums.at[1:total], sum_s, sum_r, (row, cols[1]))
         everything.wait_send()
         everything.wait_recv()
-        line = tree([sums[at, d] for d in range(total)])
-        spot = lane - iota((count, LANES), 0)
-        return [jnp.sum(jnp.where(spot == k * count, line, 0.0), axis=1, keepdims=True) for k in range(many)]
-
-    def z_dot(g4, at4):
-        z = dot(xbf[:, lanes_at(at4, 256)], v_big[lanes_at(at4, 256), :])
-        g, side = g4
-        zbuf[g, :, side * LANES:(side + 1) * LANES] = z.astype(BF16)
+        return tree([sums[d] for d in range(total)])
+
+    def z_dot(tiles_bf, at4):
+        return dot(jnp.concatenate(tiles_bf, axis=1), v_big[lanes_at(at4, 256), :]).astype(BF16)
 
     def z_copy(at, s):
         return remote(zbuf.at[cols[s]], zrecv.at[at, s], z_s.at[at, s], z_r.at[at, s], (row, cols[s]))
@@ -243,8 +281,7 @@
         return remote(tbuf.at[rows[s]], trecv.at[at, s], t_s.at[at, s], t_r.at[at, s], (rows[s], col))
 
     def halo_copy(at, side):
-        src = xbf.at[:, width - edge:width] if side == 0 else xbf.at[:, 0:edge]
-        return remote(src, halo.at[at, side], halo_s.at[at, side], halo_r.at[at, side], (after_id, before_id)[side])
+        return remote(rim.at[at, side], halo.at[at, side], halo_s.at[at, side], halo_r.at[at, side], (after_id, before_id)[side])
 
     def near(b, carry):
         for k in range(PAIRS_STEP):
@@ -264,48 +301,67 @@
 
     steps = leaves // 2 // PAIRS_STEP
 
-    def operator(at, out, add, dots, follow):
-        for s in range(1, n_col):
-            z_copy(at, s).start()
-        zrecv[at, 0] = zbuf[col]
+    def take(at, field, dots):
+        accs = [jnp.zeros((count, LANES), F32) for _ in range(len(dots) + 1)]
+        for t in range(width // LANES):
+            where = slice(t * LANES, (t + 1) * LANES)
+            tile = field[:, where]
+            spread(tile, HALO + 2 * t)
+            for m, other in enumerate(dots):
+                accs[m] = accs[m] + other[:, where] * tile
+            accs[-1] = accs[-1] + tile * tile
+            for side, k in ((0, t - width // LANES + HALO // 2), (1, t)):
+                if 0 <= k < HALO // 2:
+                    rim[at, side, :, k * LANES:(k + 1) * LANES] = tile.astype(BF16)
+        for side in range(2):
+            halo_copy(at, side).start()
+        return accs
+
+    def operator(at, out):
         if at == 0:
             loads["near"].wait()
             prepare_near()
             loads["offs"].wait()
+        lax.fori_loop(1, steps - 1, near, 0)
+        for s in range(1, n_col):
+            z_copy(at, s).wait()
+        if at == 0:
+            loads["mixc"].wait()
+        for jt in range(tiles):
+            for cq in range(n_col // QUAD):
+                got = regroup(
+                    [
+                        zrecv[at, col_slot(cq * QUAD + c4), :, jt * LANES:(jt + 1) * LANES].astype(F32)
+                        for c4 in range(QUAD)
+                    ],
+                    group,
+                )
+                for j4 in range(QUAD):
+                    left_c[jt * QUAD + j4, :, cq * LANES:(cq + 1) * LANES] = got[j4].astype(BF16)
+        for first in range(0, n_row, T_GROUP):
+            ready = (row_order + [0])[first:first + T_GROUP]
+            for s in ready:
+                made = dot(left_c[rows[s]], mixc[rows[s]]).astype(BF16)
+                if s:
+                    tbuf[rows[s]] = made
+                else:
+                    trecv[at, 0] = made
+            for s in ready:
+                if s:
+                    t_copy(at, s).start()
+        if at == 1:
+            group_start(1, group_finish(0))
+        if at == 0:
+            loads["u"].wait()
+            prepare_u()
         for side in range(2):
             halo_copy(at, side).wait()
         for side, beyond, first in ((0, me == 0, 0), (1, me == total - 1, leaves + HALO)):
             for k in range(HALO // 2):
                 tile = halo[at, side, :, k * LANES:(k + 1) * LANES].astype(F32)
                 spread(jnp.where(beyond, 0.0, tile), first + 2 * k)
-        split = steps // 4 if at == 0 else steps // 2
-        lax.fori_loop(0, split, near, 0)
-        for s in range(1, n_col):
-            z_copy(at, s).wait()
-        if at == 0:
-            loads["mixc"].wait()
-        for jt in range(tiles):
-            lefts = [[] for _ in range(QUAD)]
-            for cq in range(n_col // QUAD):
-                got = regroup(
-                    [
-                        zrecv[at, lax.rem(col + n_col - (cq * QUAD + c4), n_col), :, jt * LANES:(jt + 1) * LANES].astype(F32)
-                        for c4 in range(QUAD)
-                    ],
-                    group,
-                )
-                for j4 in range(QUAD):
-                    lefts[j4].append(got[j4].astype(BF16))
-            for j4 in range(QUAD):
-                j = jt * QUAD + j4
-                tbuf[j] = dot(jnp.concatenate(lefts[j4], axis=1), mixc[j]).astype(BF16)
-        for s in range(1, n_row):
-            t_copy(at, s).start()
-        trecv[at, 0] = tbuf[row]
-        if at == 0:
-            loads["u"].wait()
-            prepare_u()
-        lax.fori_loop(split, steps, near, 0)
+        for b in (0, steps - 1):
+            near(b, 0)
         for s in range(1, n_row):
             t_copy(at, s).wait()
         if at == 0:
@@ -314,34 +370,44 @@
             for rq in range(n_row // QUAD):
                 got = regroup(
                     [
-                        trecv[at, lax.rem(row + n_row - (rq * QUAD + r4), n_row), :, pq * LANES:(pq + 1) * LANES].astype(F32)
+                        trecv[at, row_slot(rq * QUAD + r4), :, pq * LANES:(pq + 1) * LANES].astype(F32)
                         for r4 in range(QUAD)
                     ],
                     group,
                 )
                 for p4 in range(QUAD):
                     left_r[pq * QUAD + p4, :, rq * LANES:(rq + 1) * LANES] = got[p4].astype(BF16)
-        accs = [jnp.zeros((count, LANES), F32) for _ in range(len(dots) + 1)]
-        for s in range(1, n_col + 1):
-            p = cols[s % n_col]
-            second = dot(left_r[p], mixr[p]).astype(BF16)
-            for tt in range(n_row // QUAD):
-                at4 = p * (n_row // QUAD) + tt
-                far = dot(second[:, tt * LANES:(tt + 1) * LANES], u_big[lanes_at(at4, LANES), :])
-                for k in range(2):
-                    where = lanes_at(at4 * 2 + k, LANES)
-                    image = nacc[:, where] + far[:, k * LANES:(k + 1) * LANES]
-                    if add is not None:
-                        image = add[:, where] + image
-                    out[:, where] = image
-                    for m, other in enumerate(dots):
-                        accs[m] = accs[m] + other[:, where] * image
-                    accs[-1] = accs[-1] + image * image
-                    if follow:
-                        xbf[:, where] = image.astype(BF16)
-                        spread(image, HALO + (at4 * 2 + k) * 2)
-                if follow:
-                    z_dot((p, tt), at4)
+        accs = [jnp.zeros((count, LANES), F32) for _ in range(3)]
+        for first in range(0, n_col, Z_GROUP):
+            ready = (col_order + [0])[first:first + Z_GROUP]
+            for s in ready:
+                p = cols[s]
+                second = dot(left_r[p], mixr[p]).astype(BF16)
+                for tt in range(tiles):
+                    at4 = p * tiles + tt
+                    far = dot(second[:, tt * LANES:(tt + 1) * LANES], u_big[lanes_at(at4, LANES), :])
+                    made = []
+                    for k in range(2):
+                        where = lanes_at(at4 * 2 + k, LANES)
+                        image = nacc[:, where] + far[:, k * LANES:(k + 1) * LANES]
+                        if at == 1:
+                            x_tile = x[:, where]
+                            image = x_tile + image
+                            for m, other in enumerate((rhs[:, where], x_tile, image)):
+                                accs[m] = accs[m] + other * image
+                        else:
+                            made.append(image.astype(BF16))
+                        out[:, where] = image
+                    if at == 0:
+                        z = z_dot(made, at4)
+                        if s:
+                            zbuf[p, :, tt * LANES:(tt + 1) * LANES] = z
+                        else:
+                            zrecv[1, 0, :, tt * LANES:(tt + 1) * LANES] = z
+            if at == 0:
+                for s in ready:
+                    if s:
+                        z_copy(1, s).start()
         return accs
 
     loads["v"].wait()
@@ -349,26 +415,22 @@
         loads[name].start()
     prepare_v()
     loads["rhs"].wait()
-    norm = jnp.zeros((count, LANES), F32)
-    for t in range(width // LANES):
-        tile = rhs[:, t * LANES:(t + 1) * LANES]
-        xbf[:, t * LANES:(t + 1) * LANES] = tile.astype(BF16)
-        spread(tile, HALO + 2 * t)
-        norm = norm + tile * tile
-        if t % 2:
-            g4 = t // 2
-            z_dot((g4 // tiles, g4 % tiles), g4)
-    pl.semaphore_wait(barrier, total - 1)
-    for side in range(2):
-        halo_copy(0, side).start()
-    first = operator(0, x, None, (rhs,), True)
-    for side in range(2):
-        halo_copy(1, side).start()
-    sum_start(0, [norm] + first)
-    second = operator(1, y, x, (rhs, x), False)
-    sum_start(1, second)
-    rr, rx, xx = sum_finish(0, 3)
-    ry, xy, yy = sum_finish(1, 3)
+    for g4 in range(leaves // QUAD):
+        made = [rhs[:, t * LANES:(t + 1) * LANES].astype(BF16) for t in (2 * g4, 2 * g4 + 1)]
+        zbuf[g4 // tiles, :, g4 % tiles * LANES:(g4 % tiles + 1) * LANES] = z_dot(made, g4)
+    pl.semaphore_wait(barrier, len(greeted))
+    for s in col_order:
+        z_copy(0, s).start()
+    zrecv[0, 0] = zbuf[col]
+    norm = take(0, rhs, ())
+    operator(0, x)
+    first = take(1, x, (rhs,))
+    early_line = line_of(norm + first)
+    group_start(0, early_line)
+    second = operator(1, y)
+    sum_start(line_of(second))
+    rr, rx, xx = columns_of(group_finish(1), 3)
+    ry, xy, yy = columns_of(sum_finish(), 3)
 
     beta = jnp.sqrt(rr)
     d = rx / rr
@@ -453,17 +515,19 @@
             vmem((LANES, 256), BF16),
             vmem((256, 256), BF16),
             vmem((256, 256), BF16),
-            vmem((count, width), BF16),
+            vmem((2, 2, count, HALO * LEAF), BF16),
             vmem((leaves + 2 * HALO, count, LANES), BF16),
             vmem((count, width), F32),
+            vmem((slots, count, n_col * RANK), BF16),
             vmem((n_col, count, n_row * RANK), BF16),
             vmem((n_col, count, slots * RANK), BF16),
             vmem((2, n_col, count, slots * RANK), BF16),
             vmem((n_row, count, n_col * RANK), BF16),
             vmem((2, n_row, count, n_col * RANK), BF16),
             vmem((2, 2, count, HALO * LEAF), BF16),
-            vmem((2, 1, LANES), F32),
-            vmem((2, total, 1, LANES), F32),
+            vmem((3, 1, LANES), F32),
+            vmem((2, n_col, 1, LANES), F32),
+            vmem((total, 1, LANES), F32),
             dma((7,)),
             dma((2, 2)),
             dma((2, 2)),
@@ -471,8 +535,10 @@
             dma((2, n_col)),
             dma((2, n_row)),
             dma((2, n_row)),
-            dma((2,)),
-            dma((2,)),
+            dma((2, n_col)),
+            dma((2, n_col)),
+            dma(()),
+            dma(()),
         ],
         compiler_params=pltpu.CompilerParams(
             collective_id=0, has_side_effects=True, vmem_limit_bytes=34 * 1024 * 1024

time: 49.2 us -> 44.2 us (0.90)
  Pallas kernels: 48.5 us -> 43.4 us
    pallas_call x1, Pallas kernels: 47 us -> 42 us  [body(): pl.pallas_call(kernel, out_shape=(field, field, field, jax.ShapeDtypeStru...]
where the time goes in v2:
time: 44.2 us; the launch traced here: 44.1 us
  Pallas kernels  43.4 us (98%)
  between operations  0.64 us (1%)
    pallas_call x1, Pallas kernels, body(): pl.pallas_call(kernel, out_shape=(field, field, field, jax.ShapeDtypeStru...  42 us
    pallas_call x1, Pallas kernels, body(): pl.pallas_call(finish, out_shape=(field, field), in_specs=[vmem_spec] * 4...  1.43 us

profile of v2, /device:TPU:1, one launch (start us, length us, event | category | flops | bytes accessed | tf_op | source)
XLA Modules:
  0.0 44.1 jit_solution(6261130981296896092)
XLA Ops:
  0.6 42.0 %gmres.1 = (f32[32,8192]{1,0:T(8,128)S(1)}, f32[32,8192]{1,0:T(8,128)S(1)}, f32[32,8192]{1,0:T(8,128)S(1)}, f32[2,32,128]{2,1,0:T(8,128)S(1)}) custom-call(s32[4,128]{1,0:T(4,128)} %bitcast.11, f32[32,8192]{1,0:T(8,128)} %rhs_h.1, bf16[16384,128]{1,0:T(8,128)(2,1)} %bitcast.8, bf16[128,2048]{1,0:T(8,128)(2,1)} %v_h.1, bf16[8,512,512]{2,1,0:T(8,128)(2,1)} %bitcast.9, ...), custom_call_target="tpu_custom_call" | custom-call | tf_op jit(solution)/shard_map/gmres/pallas_call | solution.py:500
  42.7 1.4 %combine.1 = (f32[32,8192]{1,0:T(8,128)}, f32[32,8192]{1,0:T(8,128)}) custom-call(f32[2,32,128]{2,1,0:T(8,128)S(1)} %get-tuple-element.6.coef, f32[32,8192]{1,0:T(8,128)S(1)} %get-tuple-element.7.rhs, f32[32,8192]{1,0:T(8,128)S(1)} %get-tuple-element.8.x, f32[32,8192]{1,0:T(8,128)S(1)} %get-tuple-element.9.y), custom_call_target="tpu_custom_call" | custom-call | tf_op jit(solution)/shard_map/combine/pallas_call | solution.py:548

commit v3 on v2

--- a/solution.py
+++ b/solution.py
@@ -11,8 +11,6 @@
 LANES = 128
 QUAD = LANES // RANK
 PAIRS_STEP = 16
-T_GROUP = 4
-Z_GROUP = 16
 RING = 4
 BF16 = jnp.bfloat16
 F32 = jnp.float32
@@ -57,7 +55,7 @@
     offs_h, rhs_h, near_h, v_h, mixc_h, mixr_h, u_h, rhs, x, y, coef,
     offs, near_raw, v_raw, mixc, mixr, u_raw,
     near_w, v_big, u_big, pick_near, pick_v, pick_u,
-    rim, xdup, nacc, left_c, left_r,
+    rim, xdup, nacc, left_c, left_r, right,
     zbuf, zrecv, tbuf, trecv, halo, part, early, sums,
     load_sem, halo_s, halo_r, z_s, z_r, t_s, t_r, early_s, early_r, sum_s, sum_r,
 ):
@@ -110,6 +108,12 @@
 
     row_far = [2 * away(i // cores) + i % cores for i in range(n_row)]
     col_far = [2 * (away(j // RING) + away(j % RING)) for j in range(n_col)]
+    odd = lax.rem(place_x, 2)
+    halves = (1 - place_x // 2, place_x // 2)
+    targets = (
+        ((2, 0), (2, 1), (3 - 2 * odd, 0), (3 - 2 * odd, 1)),
+        ((1 + 2 * odd, 0), (1 + 2 * odd, 1), (0, 1), (None, 0)),
+    )
     row_order = sorted(range(1, n_row), key=lambda i: -row_far[i])
     col_order = sorted(range(1, n_col), key=lambda j: -col_far[j])
     others = [(i, j) for i in range(n_row) for j in range(n_col) if i or j]
@@ -271,14 +275,25 @@
         everything.wait_recv()
         return tree([sums[d] for d in range(total)])
 
-    def z_dot(tiles_bf, at4):
-        return dot(jnp.concatenate(tiles_bf, axis=1), v_big[lanes_at(at4, 256), :]).astype(BF16)
-
-    def z_copy(at, s):
-        return remote(zbuf.at[cols[s]], zrecv.at[at, s], z_s.at[at, s], z_r.at[at, s], (row, cols[s]))
-
-    def t_copy(at, s):
-        return remote(tbuf.at[rows[s]], trecv.at[at, s], t_s.at[at, s], t_r.at[at, s], (rows[s], col))
+    def z_pass(at, h, field):
+        for s in col_order + [0]:
+            at4 = cols[s] * tiles + halves[h]
+            made = jnp.concatenate(
+                [field[:, lanes_at(at4 * 2 + k, LANES)].astype(BF16) for k in range(2)], axis=1
+            )
+            z = dot(made, v_big[lanes_at(at4, 256), :]).astype(BF16)
+            if s:
+                zbuf[h, cols[s]] = z
+            else:
+                zrecv[at, h, 0] = z
+
+    def z_copy(at, h, s):
+        return remote(
+            zbuf.at[h, cols[s]], zrecv.at[at, h, s], z_s.at[at, h, s], z_r.at[at, h, s], (row, cols[s])
+        )
+
+    def t_copy(at, s, to):
+        return remote(tbuf.at[to], trecv.at[at, s], t_s.at[at, s], t_r.at[at, s], (to, col))
 
     def halo_copy(at, side):
         return remote(rim.at[at, side], halo.at[at, side], halo_s.at[at, side], halo_r.at[at, side], (after_id, before_id)[side])
@@ -323,32 +338,26 @@
             prepare_near()
             loads["offs"].wait()
         lax.fori_loop(1, steps - 1, near, 0)
-        for s in range(1, n_col):
-            z_copy(at, s).wait()
-        if at == 0:
-            loads["mixc"].wait()
-        for jt in range(tiles):
+        for h in range(2):
+            for s in range(1, n_col):
+                z_copy(at, h, s).wait()
+            if at == 0 and h == 0:
+                loads["mixc"].wait()
             for cq in range(n_col // QUAD):
-                got = regroup(
-                    [
-                        zrecv[at, col_slot(cq * QUAD + c4), :, jt * LANES:(jt + 1) * LANES].astype(F32)
-                        for c4 in range(QUAD)
-                    ],
-                    group,
-                )
+                got = regroup([zrecv[at, h, col_slot(cq * QUAD + c4)].astype(F32) for c4 in range(QUAD)], group)
                 for j4 in range(QUAD):
-                    left_c[jt * QUAD + j4, :, cq * LANES:(cq + 1) * LANES] = got[j4].astype(BF16)
-        for first in range(0, n_row, T_GROUP):
-            ready = (row_order + [0])[first:first + T_GROUP]
-            for s in ready:
-                made = dot(left_c[rows[s]], mixc[rows[s]]).astype(BF16)
-                if s:
-                    tbuf[rows[s]] = made
+                    left_c[h, j4, :, cq * LANES:(cq + 1) * LANES] = got[j4].astype(BF16)
+            ready = []
+            for dx, dc in targets[h]:
+                to = lax.rem(place_x + (0 if dx is None else dx), RING) * cores + turn(place_core, dc, cores)
+                made = dot(left_c[h, lax.rem(to, QUAD)], mixc[to]).astype(BF16)
+                if dx is None:
+                    trecv[at, 0] = made
                 else:
-                    trecv[at, 0] = made
-            for s in ready:
-                if s:
-                    t_copy(at, s).start()
+                    tbuf[to] = made
+                    ready.append((dx * cores + dc, to))
+            for s, to in ready:
+                t_copy(at, s, to).start()
         if at == 1:
             group_start(1, group_finish(0))
         if at == 0:
@@ -363,7 +372,7 @@
         for b in (0, steps - 1):
             near(b, 0)
         for s in range(1, n_row):
-            t_copy(at, s).wait()
+            t_copy(at, s, rows[s]).wait()
         if at == 0:
             loads["mixr"].wait()
         for pq in range(n_col // QUAD):
@@ -377,37 +386,22 @@
                 )
                 for p4 in range(QUAD):
                     left_r[pq * QUAD + p4, :, rq * LANES:(rq + 1) * LANES] = got[p4].astype(BF16)
+        for p in range(n_col):
+            right[p] = dot(left_r[p], mixr[p]).astype(BF16)
         accs = [jnp.zeros((count, LANES), F32) for _ in range(3)]
-        for first in range(0, n_col, Z_GROUP):
-            ready = (col_order + [0])[first:first + Z_GROUP]
-            for s in ready:
-                p = cols[s]
-                second = dot(left_r[p], mixr[p]).astype(BF16)
-                for tt in range(tiles):
-                    at4 = p * tiles + tt
-                    far = dot(second[:, tt * LANES:(tt + 1) * LANES], u_big[lanes_at(at4, LANES), :])
-                    made = []
-                    for k in range(2):
-                        where = lanes_at(at4 * 2 + k, LANES)
-                        image = nacc[:, where] + far[:, k * LANES:(k + 1) * LANES]
-                        if at == 1:
-                            x_tile = x[:, where]
-                            image = x_tile + image
-                            for m, other in enumerate((rhs[:, where], x_tile, image)):
-                                accs[m] = accs[m] + other * image
-                        else:
-                            made.append(image.astype(BF16))
-                        out[:, where] = image
-                    if at == 0:
-                        z = z_dot(made, at4)
-                        if s:
-                            zbuf[p, :, tt * LANES:(tt + 1) * LANES] = z
-                        else:
-                            zrecv[1, 0, :, tt * LANES:(tt + 1) * LANES] = z
-            if at == 0:
-                for s in ready:
-                    if s:
-                        z_copy(1, s).start()
+        for p in range(n_col):
+            for tt in range(tiles):
+                at4 = p * tiles + tt
+                far = dot(right[p, :, tt * LANES:(tt + 1) * LANES], u_big[at4 * LANES:(at4 + 1) * LANES, :])
+                for k in range(2):
+                    where = slice((at4 * 2 + k) * LANES, (at4 * 2 + k + 1) * LANES)
+                    image = nacc[:, where] + far[:, k * LANES:(k + 1) * LANES]
+                    if at == 1:
+                        x_tile = x[:, where]
+                        image = x_tile + image
+                        for m, other in enumerate((rhs[:, where], x_tile, image)):
+                            accs[m] = accs[m] + other * image
+                    out[:, where] = image
         return accs
 
     loads["v"].wait()
@@ -415,15 +409,18 @@
         loads[name].start()
     prepare_v()
     loads["rhs"].wait()
-    for g4 in range(leaves // QUAD):
-        made = [rhs[:, t * LANES:(t + 1) * LANES].astype(BF16) for t in (2 * g4, 2 * g4 + 1)]
-        zbuf[g4 // tiles, :, g4 % tiles * LANES:(g4 % tiles + 1) * LANES] = z_dot(made, g4)
+    for h in range(2):
+        z_pass(0, h, rhs)
     pl.semaphore_wait(barrier, len(greeted))
-    for s in col_order:
-        z_copy(0, s).start()
-    zrecv[0, 0] = zbuf[col]
+    for h in range(2):
+        for s in col_order:
+            z_copy(0, h, s).start()
     norm = take(0, rhs, ())
     operator(0, x)
+    for h in range(2):
+        z_pass(1, h, x)
+        for s in col_order:
+            z_copy(1, h, s).start()
     first = take(1, x, (rhs,))
     early_line = line_of(norm + first)
     group_start(0, early_line)
@@ -518,10 +515,11 @@
             vmem((2, 2, count, HALO * LEAF), BF16),
             vmem((leaves + 2 * HALO, count, LANES), BF16),
             vmem((count, width), F32),
-            vmem((slots, count, n_col * RANK), BF16),
+            vmem((2, QUAD, count, n_col * RANK), BF16),
             vmem((n_col, count, n_row * RANK), BF16),
-            vmem((n_col, count, slots * RANK), BF16),
-            vmem((2, n_col, count, slots * RANK), BF16),
+            vmem((n_col, count, n_row * RANK), BF16),
+            vmem((2, n_col, count, LANES), BF16),
+            vmem((2, 2, n_col, count, LANES), BF16),
             vmem((n_row, count, n_col * RANK), BF16),
             vmem((2, n_row, count, n_col * RANK), BF16),
             vmem((2, 2, count, HALO * LEAF), BF16),
@@ -531,8 +529,8 @@
             dma((7,)),
             dma((2, 2)),
             dma((2, 2)),
-            dma((2, n_col)),
-            dma((2, n_col)),
+            dma((2, 2, n_col)),
+            dma((2, 2, n_col)),
             dma((2, n_row)),
             dma((2, n_row)),
             dma((2, n_col)),

time: 44.2 us -> 40.6 us (0.919)
  Pallas kernels: 43.4 us -> 39.9 us
    pallas_call x1, Pallas kernels: 42 us -> 38.4 us  [body(): pl.pallas_call(kernel, out_shape=(field, field, field, jax.ShapeDtypeStru...]
where the time goes in v3:
time: 40.6 us; the launch traced here: 40.5 us
  Pallas kernels  39.9 us (98%)
  between operations  0.64 us (2%)
    pallas_call x1, Pallas kernels, body(): pl.pallas_call(kernel, out_shape=(field, field, field, jax.ShapeDtypeStru...  38.4 us
    pallas_call x1, Pallas kernels, body(): pl.pallas_call(finish, out_shape=(field, field), in_specs=[vmem_spec] * 4...  1.43 us

profile of v3, /device:TPU:1, one launch (start us, length us, event | category | flops | bytes accessed | tf_op | source)
XLA Modules:
  0.0 40.5 jit_solution(15536526000736040304)
XLA Ops:
  0.6 38.4 %gmres.1 = (f32[32,8192]{1,0:T(8,128)S(1)}, f32[32,8192]{1,0:T(8,128)S(1)}, f32[32,8192]{1,0:T(8,128)S(1)}, f32[2,32,128]{2,1,0:T(8,128)S(1)}) custom-call(s32[4,128]{1,0:T(4,128)} %bitcast.11, f32[32,8192]{1,0:T(8,128)} %rhs_h.1, bf16[16384,128]{1,0:T(8,128)(2,1)} %bitcast.8, bf16[128,2048]{1,0:T(8,128)(2,1)} %v_h.1, bf16[8,512,512]{2,1,0:T(8,128)(2,1)} %bitcast.9, ...), custom_call_target="tpu_custom_call" | custom-call | tf_op jit(solution)/shard_map/gmres/pallas_call | solution.py:497
  39.1 1.4 %combine.1 = (f32[32,8192]{1,0:T(8,128)}, f32[32,8192]{1,0:T(8,128)}) custom-call(f32[2,32,128]{2,1,0:T(8,128)S(1)} %get-tuple-element.6.coef, f32[32,8192]{1,0:T(8,128)S(1)} %get-tuple-element.7.rhs, f32[32,8192]{1,0:T(8,128)S(1)} %get-tuple-element.8.x, f32[32,8192]{1,0:T(8,128)S(1)} %get-tuple-element.9.y), custom_call_target="tpu_custom_call" | custom-call | tf_op jit(solution)/shard_map/combine/pallas_call | solution.py:546

commit v4 on v3

--- a/solution.py
+++ b/solution.py
@@ -11,6 +11,7 @@
 LANES = 128
 QUAD = LANES // RANK
 PAIRS_STEP = 16
+PREPARE_STEP = 32
 RING = 4
 BF16 = jnp.bfloat16
 F32 = jnp.float32
@@ -55,7 +56,7 @@
     offs_h, rhs_h, near_h, v_h, mixc_h, mixr_h, u_h, rhs, x, y, coef,
     offs, near_raw, v_raw, mixc, mixr, u_raw,
     near_w, v_big, u_big, pick_near, pick_v, pick_u,
-    rim, xdup, nacc, left_c, left_r, right,
+    rim, xdup, nacc, left_c, left_r, right, z_mid, z_mix, z_near,
     zbuf, zrecv, tbuf, trecv, halo, part, early, sums,
     load_sem, halo_s, halo_r, z_s, z_r, t_s, t_r, early_s, early_r, sum_s, sum_r,
 ):
@@ -147,13 +148,14 @@
     def prepare_v():
         lane16 = iota((16, LANES), 1) // RANK
         place = lane16 == iota((16, LANES), 0) % QUAD
+        blank = jnp.zeros((16, LANES), BF16)
         for b in range(leaves // 32):
             sides = []
             for h in range(2):
                 base = b * 32 + h * 16
-                raw = [v_raw[base:base + 16, t * LANES:(t + 1) * LANES].astype(F32) for t in range(16)]
+                raw = [v_raw[base:base + 16, t * LANES:(t + 1) * LANES] for t in range(16)]
                 sides.append(
-                    [[jnp.where(place, turned(a, d * RANK), 0.0).astype(BF16) for a in raw] for d in range(4)]
+                    [[jnp.where(place, turned(a, d * RANK), blank) for a in raw] for d in range(4)]
                 )
             for q in range(4):
                 both = jnp.concatenate(
@@ -177,9 +179,9 @@
             sides = []
             for h in range(2):
                 base = b * 32 + h * 16
-                raw = [u_raw[base:base + 16, t * LANES:(t + 1) * LANES].astype(F32) for t in range(16)]
+                raw = [u_raw[base:base + 16, t * LANES:(t + 1) * LANES] for t in range(16)]
                 sides.append(
-                    [[jnp.where(place, turned(a, d * LEAF), 0.0).astype(BF16) for a in raw] for d in range(2)]
+                    [[jnp.where(place, turned(a, d * LEAF), blank) for a in raw] for d in range(2)]
                 )
             for q in range(2):
                 both = jnp.concatenate(
@@ -203,8 +205,8 @@
         keep = (iota((size, LANES), 1) // LEAF) == iota((size, LANES), 0) % 2
 
         def block(b, carry):
-            for k in range(PAIRS_STEP):
-                pair = b * PAIRS_STEP + k
+            for k in range(PREPARE_STEP):
+                pair = b * PREPARE_STEP + k
                 sides = []
                 for h in range(2):
                     raw = near_raw[lanes_at(pair * 2 + h, size), :].astype(F32)
@@ -225,12 +227,12 @@
                         ].astype(BF16)
             return carry
 
-        lax.fori_loop(0, leaves // 2 // PAIRS_STEP, block, 0)
+        lax.fori_loop(0, leaves // 2 // PREPARE_STEP, block, 0)
 
     def spread(tile, first):
         swapped = pltpu.roll(tile, LEAF, 1)
-        xdup[first] = jnp.where(low, tile, swapped).astype(BF16)
-        xdup[first + 1] = jnp.where(low, swapped, tile).astype(BF16)
+        xdup[first] = jnp.where(low, tile, swapped)
+        xdup[first + 1] = jnp.where(low, swapped, tile)
 
     def remote(src, dst, send, recv, to):
         return pltpu.make_async_remote_copy(
@@ -274,6 +276,33 @@
         everything.wait_send()
         everything.wait_recv()
         return tree([sums[d] for d in range(total)])
+
+    def prepare_z():
+        blank = jnp.zeros((LANES, LANES), BF16)
+
+        for at4 in range(leaves // QUAD):
+            p, tt = at4 // tiles, at4 % tiles
+            made = dot(u_big[at4 * LANES:(at4 + 1) * LANES, :], v_big[at4 * 256:(at4 + 1) * 256, :]).astype(BF16)
+            rows_of = slice(tt * LANES, (tt + 1) * LANES)
+            z_mid[p, rows_of, rows_of] = made
+            z_mid[p, rows_of, (1 - tt) * LANES:(2 - tt) * LANES] = blank
+        for p in range(n_col):
+            made = dot(mixr[p], z_mid[p]).astype(BF16)
+            for tt in range(tiles):
+                z_mix[tt, p] = made[:, tt * LANES:(tt + 1) * LANES]
+
+    def near_z():
+        for g4 in range(leaves // QUAD):
+            made = nacc[:, g4 * 256:(g4 + 1) * 256].astype(BF16)
+            z_near[g4] = dot(made, v_big[g4 * 256:(g4 + 1) * 256, :])
+
+    def z_mixed(h):
+        for s in col_order + [0]:
+            z = dot(left_r[cols[s]], z_mix[halves[h], cols[s]]) + z_near[cols[s] * tiles + halves[h]]
+            if s:
+                zbuf[h, cols[s]] = z.astype(BF16)
+            else:
+                zrecv[1, h, 0] = z.astype(BF16)
 
     def z_pass(at, h, field):
         for s in col_order + [0]:
@@ -321,13 +350,14 @@
         for t in range(width // LANES):
             where = slice(t * LANES, (t + 1) * LANES)
             tile = field[:, where]
-            spread(tile, HALO + 2 * t)
+            rounded = tile.astype(BF16)
+            spread(rounded, HALO + 2 * t)
             for m, other in enumerate(dots):
                 accs[m] = accs[m] + other[:, where] * tile
             accs[-1] = accs[-1] + tile * tile
             for side, k in ((0, t - width // LANES + HALO // 2), (1, t)):
                 if 0 <= k < HALO // 2:
-                    rim[at, side, :, k * LANES:(k + 1) * LANES] = tile.astype(BF16)
+                    rim[at, side, :, k * LANES:(k + 1) * LANES] = rounded
         for side in range(2):
             halo_copy(at, side).start()
         return accs
@@ -338,17 +368,24 @@
             prepare_near()
             loads["offs"].wait()
         lax.fori_loop(1, steps - 1, near, 0)
+        if at == 0:
+            loads["u"].wait()
+            prepare_u()
         for h in range(2):
             for s in range(1, n_col):
                 z_copy(at, h, s).wait()
             if at == 0 and h == 0:
                 loads["mixc"].wait()
             for cq in range(n_col // QUAD):
-                got = regroup([zrecv[at, h, col_slot(cq * QUAD + c4)].astype(F32) for c4 in range(QUAD)], group)
+                got = regroup([zrecv[at, h, col_slot(cq * QUAD + c4)] for c4 in range(QUAD)], group)
                 for j4 in range(QUAD):
-                    left_c[h, j4, :, cq * LANES:(cq + 1) * LANES] = got[j4].astype(BF16)
+                    left_c[h, j4, :, cq * LANES:(cq + 1) * LANES] = got[j4]
             ready = []
             for dx, dc in targets[h]:
+                if len(ready) == 2:
+                    for s, to in ready:
+                        t_copy(at, s, to).start()
+                    ready = []
                 to = lax.rem(place_x + (0 if dx is None else dx), RING) * cores + turn(place_core, dc, cores)
                 made = dot(left_c[h, lax.rem(to, QUAD)], mixc[to]).astype(BF16)
                 if dx is None:
@@ -361,31 +398,36 @@
         if at == 1:
             group_start(1, group_finish(0))
         if at == 0:
-            loads["u"].wait()
-            prepare_u()
+            loads["mixr"].wait()
+            prepare_z()
         for side in range(2):
             halo_copy(at, side).wait()
         for side, beyond, first in ((0, me == 0, 0), (1, me == total - 1, leaves + HALO)):
             for k in range(HALO // 2):
-                tile = halo[at, side, :, k * LANES:(k + 1) * LANES].astype(F32)
-                spread(jnp.where(beyond, 0.0, tile), first + 2 * k)
+                tile = halo[at, side, :, k * LANES:(k + 1) * LANES]
+                spread(jnp.where(beyond, jnp.zeros_like(tile), tile), first + 2 * k)
         for b in (0, steps - 1):
             near(b, 0)
+        if at == 0:
+            near_z()
         for s in range(1, n_row):
             t_copy(at, s, rows[s]).wait()
-        if at == 0:
-            loads["mixr"].wait()
         for pq in range(n_col // QUAD):
             for rq in range(n_row // QUAD):
                 got = regroup(
                     [
-                        trecv[at, row_slot(rq * QUAD + r4), :, pq * LANES:(pq + 1) * LANES].astype(F32)
+                        trecv[at, row_slot(rq * QUAD + r4), :, pq * LANES:(pq + 1) * LANES]
                         for r4 in range(QUAD)
                     ],
                     group,
                 )
                 for p4 in range(QUAD):
-                    left_r[pq * QUAD + p4, :, rq * LANES:(rq + 1) * LANES] = got[p4].astype(BF16)
+                    left_r[pq * QUAD + p4, :, rq * LANES:(rq + 1) * LANES] = got[p4]
+        if at == 0:
+            for h in range(2):
+                z_mixed(h)
+                for s in col_order:
+                    z_copy(1, h, s).start()
         for p in range(n_col):
             right[p] = dot(left_r[p], mixr[p]).astype(BF16)
         accs = [jnp.zeros((count, LANES), F32) for _ in range(3)]
@@ -417,10 +459,6 @@
             z_copy(0, h, s).start()
     norm = take(0, rhs, ())
     operator(0, x)
-    for h in range(2):
-        z_pass(1, h, x)
-        for s in col_order:
-            z_copy(1, h, s).start()
     first = take(1, x, (rhs,))
     early_line = line_of(norm + first)
     group_start(0, early_line)
@@ -518,6 +556,9 @@
             vmem((2, QUAD, count, n_col * RANK), BF16),
             vmem((n_col, count, n_row * RANK), BF16),
             vmem((n_col, count, n_row * RANK), BF16),
+            vmem((n_col, 2 * LANES, 2 * LANES), BF16),
+            vmem((2, n_col, 2 * LANES, LANES), BF16),
+            vmem((leaves // QUAD, count, LANES), F32),
             vmem((2, n_col, count, LANES), BF16),
             vmem((2, 2, n_col, count, LANES), BF16),
             vmem((n_row, count, n_col * RANK), BF16),

time: 40.6 us -> 39.8 us (0.980)
  Pallas kernels: 39.9 us -> 39.1 us
    pallas_call x1, Pallas kernels: 38.4 us -> 37.6 us  [body(): pl.pallas_call(kernel, out_shape=(field, field, field, jax.ShapeDtypeStru...]
where the time goes in v4:
time: 39.8 us; the launch traced here: 39.7 us
  Pallas kernels  39.1 us (98%)
  between operations  0.64 us (2%)
    pallas_call x1, Pallas kernels, body(): pl.pallas_call(kernel, out_shape=(field, field, field, jax.ShapeDtypeStru...  37.6 us
    pallas_call x1, Pallas kernels, body(): pl.pallas_call(finish, out_shape=(field, field), in_specs=[vmem_spec] * 4...  1.43 us

profile of v4, /device:TPU:1, one launch (start us, length us, event | category | flops | bytes accessed | tf_op | source)
XLA Modules:
  0.0 39.7 jit_solution(16475622131143489161)
XLA Ops:
  0.6 37.6 %gmres.1 = (f32[32,8192]{1,0:T(8,128)S(1)}, f32[32,8192]{1,0:T(8,128)S(1)}, f32[32,8192]{1,0:T(8,128)S(1)}, f32[2,32,128]{2,1,0:T(8,128)S(1)}) custom-call(s32[4,128]{1,0:T(4,128)} %bitcast.11, f32[32,8192]{1,0:T(8,128)} %rhs_h.1, bf16[16384,128]{1,0:T(8,128)(2,1)} %bitcast.8, bf16[128,2048]{1,0:T(8,128)(2,1)} %v_h.1, bf16[8,512,512]{2,1,0:T(8,128)(2,1)} %bitcast.9, ...), custom_call_target="tpu_custom_call" | custom-call | tf_op jit(solution)/shard_map/gmres/pallas_call | solution.py:535
  38.3 1.4 %combine.1 = (f32[32,8192]{1,0:T(8,128)}, f32[32,8192]{1,0:T(8,128)}) custom-call(f32[2,32,128]{2,1,0:T(8,128)S(1)} %get-tuple-element.6.coef, f32[32,8192]{1,0:T(8,128)S(1)} %get-tuple-element.7.rhs, f32[32,8192]{1,0:T(8,128)S(1)} %get-tuple-element.8.x, f32[32,8192]{1,0:T(8,128)S(1)} %get-tuple-element.9.y), custom_call_target="tpu_custom_call" | custom-call | tf_op jit(solution)/shard_map/combine/pallas_call | solution.py:587

commit v5 on v4

--- a/solution.py
+++ b/solution.py
@@ -489,23 +489,23 @@
     coef[1] = jnp.broadcast_to(on_x, (count, LANES))
 
 
-CHUNKS = 4
+CHUNKS = (4, 12, 16, 16, 16)
 
 
 def finish(coef, rhs, x, y, sol_h, res_h, sol, res, sem):
     count, width = rhs.shape
     on_r = coef[0]
     on_x = coef[1]
-    size = width // CHUNKS
     copies = []
-    for c in range(CHUNKS):
-        for t in range(size // LANES):
-            where = slice(c * size + t * LANES, c * size + (t + 1) * LANES)
+    for c, many in enumerate(CHUNKS):
+        first = sum(CHUNKS[:c])
+        for t in range(first, first + many):
+            where = slice(t * LANES, (t + 1) * LANES)
             r_tile = rhs[:, where]
             x_tile = x[:, where]
             sol[:, where] = on_r * r_tile + on_x * x_tile
             res[:, where] = r_tile - on_r * (r_tile + x_tile) - on_x * y[:, where]
-        span = slice(c * size, (c + 1) * size)
+        span = slice(first * LANES, (first + many) * LANES)
         for k, (src, dst) in enumerate(((sol, sol_h), (res, res_h))):
             copies.append(pltpu.make_async_copy(src.at[:, span], dst.at[:, span], sem.at[c, k]))
             copies[-1].start()
@@ -589,7 +589,7 @@
         out_shape=(field, field),
         in_specs=[vmem_spec] * 4,
         out_specs=(hbm_spec,) * 2,
-        scratch_shapes=[vmem((count, width), F32), vmem((count, width), F32), dma((CHUNKS, 2))],
+        scratch_shapes=[vmem((count, width), F32), vmem((count, width), F32), dma((len(CHUNKS), 2))],
         compiler_params=pltpu.CompilerParams(vmem_limit_bytes=16 * 1024 * 1024),
         name="combine",
     )(coef, rhs_v, x, y)

time: 39.8 us -> 39.8 us (level)
  no operation moved by 1% of the time
where the time goes in v5:
time: 39.8 us; the launch traced here: 39.7 us
  Pallas kernels  39 us (98%)
  between operations  0.64 us (2%)
    pallas_call x1, Pallas kernels, body(): pl.pallas_call(kernel, out_shape=(field, field, field, jax.ShapeDtypeStru...  37.6 us
    pallas_call x1, Pallas kernels, body(): pl.pallas_call(finish, out_shape=(field, field), in_specs=[vmem_spec] * 4...  1.41 us

profile of v5, /device:TPU:1, one launch (start us, length us, event | category | flops | bytes accessed | tf_op | source)
XLA Modules:
  0.0 39.7 jit_solution(17319708127312222032)
XLA Ops:
  0.6 37.6 %gmres.1 = (f32[32,8192]{1,0:T(8,128)S(1)}, f32[32,8192]{1,0:T(8,128)S(1)}, f32[32,8192]{1,0:T(8,128)S(1)}, f32[2,32,128]{2,1,0:T(8,128)S(1)}) custom-call(s32[4,128]{1,0:T(4,128)} %bitcast.11, f32[32,8192]{1,0:T(8,128)} %rhs_h.1, bf16[16384,128]{1,0:T(8,128)(2,1)} %bitcast.8, bf16[128,2048]{1,0:T(8,128)(2,1)} %v_h.1, bf16[8,512,512]{2,1,0:T(8,128)(2,1)} %bitcast.9, ...), custom_call_target="tpu_custom_call" | custom-call | tf_op jit(solution)/shard_map/gmres/pallas_call | solution.py:535
  38.3 1.4 %combine.1 = (f32[32,8192]{1,0:T(8,128)}, f32[32,8192]{1,0:T(8,128)}) custom-call(f32[2,32,128]{2,1,0:T(8,128)S(1)} %get-tuple-element.6.coef, f32[32,8192]{1,0:T(8,128)S(1)} %get-tuple-element.7.rhs, f32[32,8192]{1,0:T(8,128)S(1)} %get-tuple-element.8.x, f32[32,8192]{1,0:T(8,128)S(1)} %get-tuple-element.9.y), custom_call_target="tpu_custom_call" | custom-call | tf_op jit(solution)/shard_map/combine/pallas_call | solution.py:587

commit v6 on v5

--- a/solution.py
+++ b/solution.py
@@ -372,14 +372,17 @@
             loads["u"].wait()
             prepare_u()
         for h in range(2):
-            for s in range(1, n_col):
-                z_copy(at, h, s).wait()
+            for dz in (0, 1, 3, 2):
+                for dy in range(RING):
+                    if dz or dy:
+                        z_copy(at, h, dz * RING + dy).wait()
+                plane = lax.rem(place_z + RING - dz, RING)
+                slots_of = [dz * RING + lax.rem(place_y + RING - c4, RING) for c4 in range(QUAD)]
+                got = regroup([zrecv[at, h, s] for s in slots_of], group)
+                for j4 in range(QUAD):
+                    left_c[h, j4, :, lanes_at(plane, LANES)] = got[j4]
             if at == 0 and h == 0:
                 loads["mixc"].wait()
-            for cq in range(n_col // QUAD):
-                got = regroup([zrecv[at, h, col_slot(cq * QUAD + c4)] for c4 in range(QUAD)], group)
-                for j4 in range(QUAD):
-                    left_c[h, j4, :, cq * LANES:(cq + 1) * LANES] = got[j4]
             ready = []
             for dx, dc in targets[h]:
                 if len(ready) == 2:

time: 39.8 us -> 40.2 us (1.010)
  no operation moved by 1% of the time
where the time goes in v6:
time: 40.2 us; the launch traced here: 40.1 us
  Pallas kernels  39.4 us (98%)
  between operations  0.64 us (2%)
    pallas_call x1, Pallas kernels, body(): pl.pallas_call(kernel, out_shape=(field, field, field, jax.ShapeDtypeStru...  38 us
    pallas_call x1, Pallas kernels, body(): pl.pallas_call(finish, out_shape=(field, field), in_specs=[vmem_spec] * 4...  1.41 us

profile of v6, /device:TPU:1, one launch (start us, length us, event | category | flops | bytes accessed | tf_op | source)
XLA Modules:
  0.0 40.1 jit_solution(1573417968349529719)
XLA Ops:
  0.6 38.0 %gmres.1 = (f32[32,8192]{1,0:T(8,128)S(1)}, f32[32,8192]{1,0:T(8,128)S(1)}, f32[32,8192]{1,0:T(8,128)S(1)}, f32[2,32,128]{2,1,0:T(8,128)S(1)}) custom-call(s32[4,128]{1,0:T(4,128)} %bitcast.11, f32[32,8192]{1,0:T(8,128)} %rhs_h.1, bf16[16384,128]{1,0:T(8,128)(2,1)} %bitcast.8, bf16[128,2048]{1,0:T(8,128)(2,1)} %v_h.1, bf16[8,512,512]{2,1,0:T(8,128)(2,1)} %bitcast.9, ...), custom_call_target="tpu_custom_call" | custom-call | tf_op jit(solution)/shard_map/gmres/pallas_call | solution.py:538
  38.7 1.4 %combine.1 = (f32[32,8192]{1,0:T(8,128)}, f32[32,8192]{1,0:T(8,128)}) custom-call(f32[2,32,128]{2,1,0:T(8,128)S(1)} %get-tuple-element.6.coef, f32[32,8192]{1,0:T(8,128)S(1)} %get-tuple-element.7.rhs, f32[32,8192]{1,0:T(8,128)S(1)} %get-tuple-element.8.x, f32[32,8192]{1,0:T(8,128)S(1)} %get-tuple-element.9.y), custom_call_target="tpu_custom_call" | custom-call | tf_op jit(solution)/shard_map/combine/pallas_call | solution.py:590
